TPU v7x, 32 devices: a whole 2x2x4 slice. The times are simulated.
32 devices in a mesh: gx: 8 (over y, x, core), gy: 4 (over z).
Axes of the slice: x: 2, y: 2, z: 4, core: 2. Of those that a mesh axis runs over, the one named last changes fastest.
Arguments:
- terminal: float32 [128, 2048], P('gx', 'gy'), may hold values from -15 to 15
- initial_density: float32 [128, 2048], P('gx', 'gy'), may hold values from 0.1 to 1
- density_guess: float32 [2, 128, 2048], P(None, 'gx', 'gy'), may hold values from 0.1 to 1
- diagonal: float32 [128, 2048], P('gx', 'gy'), may hold values from 0.1 to 2
Outputs:
- value_field: float32 [128, 2048], P('gx', 'gy')
- density_field: float32 [128, 2048], P('gx', 'gy')
All inputs are finite; a program needn't handle non-finite values.
Results may differ from a plain program's by a relative error of at most 0.00011.
Values sent between devices are 32-bit elements; how exact they have to be, the bound alone decides.
A program may use at most 64 MiB of HBM per device.

v0:
```python
import functools

import jax
import jax.numpy as jnp
from jax import lax
from jax.experimental import pallas as pl
from jax.experimental.pallas import tpu as pltpu
from jax.sharding import PartitionSpec as P

MESH = pl.DeviceIdType.MESH

LEVELS = 2
MARGIN = 16
LANES = 128

inv_step = 0.5
coupling = 0.5

SCALE = 0.25
SHIFT = 5.5

DIRECTIONS = [(r, c) for r in (-1, 0, 1) for c in (-1, 0, 1) if (r, c) != (0, 0)]
TINY = 2e-7


def solve_small(nu):
    g00 = nu[1] / SCALE + SHIFT * nu[0]
    g01 = nu[2] / SCALE + SHIFT * nu[1]
    g02 = nu[3] / SCALE + SHIFT * nu[2]
    g12 = nu[4] / SCALE + SHIFT * nu[3]
    g22 = nu[5] / SCALE + SHIFT * nu[4]
    g11 = g02
    inv0 = 1.0 / g00
    l10 = g01 * inv0
    l20 = g02 * inv0
    d1 = g11 - l10 * g01
    ok1 = d1 > TINY * g11
    inv1 = jnp.where(ok1, 1.0 / jnp.where(ok1, d1, 1.0), 0.0)
    t = g12 - l20 * g01
    l21 = t * inv1
    d2 = g22 - l20 * g02 - l21 * t
    ok2 = ok1 & (d2 > TINY * g22)
    inv2 = jnp.where(ok2, 1.0 / jnp.where(ok2, d2, 1.0), 0.0)
    y1 = nu[1] - l10 * nu[0]
    y2 = nu[2] - l20 * nu[0] - l21 * y1
    c2 = y2 * inv2
    c1 = y1 * inv1 - l21 * c2
    c0 = nu[0] * inv0 - l10 * c1 - l20 * c2
    return c0, c1, c2


def kernel(nx, ny, term_ref, dens_ref, guess_ref, diag_ref, both_ref,
           main, left, right, sent, slots, halo_send, halo_recv, own_sem, sum_send, sum_recv,
           ready, scaled_tall, scaled_mid, scaled_small):
    rows, cols = term_ref.shape
    gx = lax.axis_index("gx")
    gy = lax.axis_index("gy")
    count = nx * ny
    me = gx * ny + gy

    def inside(dr, dc):
        ok = None
        for here_at, step, size in ((gx, dr, nx), (gy, dc, ny)):
            if step == 1:
                test = here_at < size - 1
            elif step == -1:
                test = here_at > 0
            else:
                continue
            ok = test if ok is None else ok & test
        return ok

    def across(k):
        return (lax.rem(gx + k, nx), gy)

    def along(k):
        return (gx, lax.rem(gy + k, ny))

    barrier = pltpu.get_barrier_semaphore()
    greeted = nx + ny - 2
    for k in range(1, nx):
        pl.semaphore_signal(barrier, inc=1, device_id=across(k), device_id_type=MESH)
    for k in range(1, ny):
        pl.semaphore_signal(barrier, inc=1, device_id=along(k), device_id_type=MESH)
    for dr, dc in DIRECTIONS:
        if dr != 0 and dc != 0:
            there = inside(dr, dc)
            greeted = greeted + jnp.where(there, 1, 0)

            @pl.when(there)
            def _():
                pl.semaphore_signal(
                    barrier, inc=1, device_id=(gx + dr, gy + dc), device_id_type=MESH)

    here = pl.ds(MARGIN, rows)
    own = [
        pltpu.make_async_copy(source, main.at[at, here], own_sem.at[at])
        for at, source in enumerate(
            (term_ref, diag_ref, guess_ref.at[1], guess_ref.at[0], dens_ref))
    ]
    for copy in own:
        copy.start()
    wide = cols + LANES
    half = LANES // 2
    tall = rows + 2 * MARGIN
    low_mid, high_mid = MARGIN - 8, MARGIN + rows + 8

    def mask_of(size, cyclic, margin):
        row = lax.broadcasted_iota(jnp.int32, (size, wide), 0)
        col = lax.broadcasted_iota(jnp.int32, (size, wide), 1)
        col_low = jnp.where(gy < ny - 1, cols + half, cols)
        col_high = jnp.where(gy > 0, cols + half, wide)
        ok = (col < col_low) | (col >= col_high)
        if cyclic:
            row_low = jnp.where(gx < nx - 1, rows + 4, rows)
            row_high = jnp.where(gx > 0, rows + 4, size)
            return ok & ((row < row_low) | (row >= row_high))
        row_low = jnp.where(gx > 0, 0, margin)
        row_high = jnp.where(gx < nx - 1, size, margin + rows)
        return ok & (row >= row_low) & (row < row_high)

    scaled = {"tall": scaled_tall, "mid": scaled_mid, "small": scaled_small}
    scaled_tall[...] = jnp.where(mask_of(tall, False, MARGIN), SCALE, 0.0)
    scaled_mid[...] = jnp.where(mask_of(rows + 16, False, 8), SCALE, 0.0)
    scaled_small[...] = jnp.where(mask_of(rows + 8, True, 4), SCALE, 0.0)

    for copy in own:
        copy.wait()
    pl.semaphore_wait(barrier, greeted)

    def pieces(dr):
        if dr == 0:
            return [(0, 3, 0, rows), (3, 2, 0, rows)]
        return [(0, 3, 0, 8), (0, 4, 8, 8), (3, 2, 0, 8)]

    def halo(d, piece):
        dr, dc = DIRECTIONS[d]
        first, many, out, size = pieces(dr)[piece]
        if dr == 0:
            src_rows, dst_rows = here, here
        elif dr == 1:
            src_rows = pl.ds(MARGIN + rows - out - size, size)
            dst_rows = pl.ds(MARGIN - out - size, size)
        else:
            src_rows = pl.ds(MARGIN + out, size)
            dst_rows = pl.ds(MARGIN + rows + out, size)
        if dc == 0:
            src_cols, buf = pl.ds(0, cols), main
        elif dc == 1:
            src_cols, buf = pl.ds(cols - LANES, LANES), left
        else:
            src_cols, buf = pl.ds(0, LANES), right
        return pltpu.make_async_remote_copy(
            src_ref=main.at[pl.ds(first, many), src_rows, src_cols],
            dst_ref=buf.at[pl.ds(first, many), dst_rows, :],
            send_sem=halo_send.at[d, piece], recv_sem=halo_recv.at[d, piece],
            device_id=(gx + dr, gy + dc), device_id_type=MESH)

    def each_halo(near, act, back=False):
        for d, (dr, dc) in enumerate(DIRECTIONS):
            @pl.when(inside(-dr, -dc) if back else inside(dr, dc))
            def _():
                for piece in [0] if near else range(1, len(pieces(dr))):
                    act(halo(d, piece))

    each_halo(True, lambda copy: copy.start())
    for k in range(1, nx):
        pl.semaphore_signal(ready, inc=1, device_id=across(k), device_id_type=MESH)
    each_halo(False, lambda copy: copy.start())

    def shrink(x, start):
        sub = lax.broadcasted_iota(jnp.int32, (8, x.shape[1]), 0)
        ends = jnp.where(sub < 4, x[start + rows:start + rows + 8], x[start - 8:start])
        return jnp.concatenate([x[start:start + rows], ends], axis=0)

    def strip(a, begin, end):
        lane = lax.broadcasted_iota(jnp.int32, (end - begin, LANES), 1)
        edge = jnp.where(lane < half, right[a, begin:end], left[a, begin:end])
        return jnp.concatenate([main[a, begin:end], edge], axis=1)

    def field(a, window):
        if window == "tall":
            return strip(a, 0, tall)
        x = strip(a, low_mid, high_mid)
        return x if window == "mid" else shrink(x, 8)

    def up(x):
        return pltpu.roll(x, 1, 0)

    def down(x):
        return pltpu.roll(x, x.shape[0] - 1, 0)

    def before(x):
        return pltpu.roll(x, 1, 1)

    def after(x):
        return pltpu.roll(x, x.shape[1] - 1, 1)

    def masked(x, window):
        return jnp.where(scaled[window][...] > 0.0, x, 0.0)

    def core_of(window):
        return masked(SCALE * (field(1, window) + (inv_step + 4.0 - SHIFT)), window)

    def apply_b(v, core, window):
        beside = (up(v) + down(v)) + (before(v) + after(v))
        return core * v - scaled[window][...] * beside

    def apply_half(v, core):
        return (0.5 * core) * v - SCALE * (down(v) + after(v))

    def hamiltonian(u):
        dx = u - up(u)
        dy = u - before(u)
        px, qx = jnp.maximum(dx, 0.0), jnp.minimum(dx, 0.0)
        py, qy = jnp.maximum(dy, 0.0), jnp.minimum(dy, 0.0)
        return (px * px + down(qx * qx)) + (py * py + after(qy * qy))

    def faces(u):
        sx = u - down(u)
        sy = u - after(u)
        return jnp.maximum(sx, 0.0), jnp.minimum(sx, 0.0), jnp.maximum(sy, 0.0), jnp.minimum(sy, 0.0)

    def advance(m, face, window):
        px, qx, py, qy = face
        fx = px * m + qx * down(m)
        fy = py * m + qy * after(m)
        net = (fx - up(fx)) + (fy - before(fy))
        return scaled[window][...] * ((inv_step / SCALE) * m - (1.0 / SCALE) * net)

    def value_rhs(later, level, window):
        guess = masked(coupling * field(2 if level == 1 else 3, window), window)
        own_part = (inv_step / SCALE) * later - (0.5 / SCALE) * hamiltonian(later)
        return scaled[window][...] * own_part + guess

    def fold(p):
        parts = [p[i:i + 8, j:j + LANES] for i in range(0, rows, 8) for j in range(0, cols, LANES)]
        while len(parts) > 1:
            odd = parts[len(parts) // 2 * 2:]
            parts = [parts[i] + parts[i + 1] for i in range(0, len(parts) - 1, 2)] + odd
        return parts[0]

    def dot(x, y):
        return fold(x * y)

    sub8 = lax.broadcasted_iota(jnp.int32, (8, LANES), 0)
    lane8 = lax.broadcasted_iota(jnp.int32, (8, LANES), 1)

    def pack(tiles):
        spread = None
        for first in range(0, len(tiles), 8):
            group = tiles[first:first + 8]
            group = group + [jnp.zeros((8, LANES), jnp.float32)] * (8 - len(group))
            for step in (4, 2, 1):
                keep = lax.rem(sub8, 2 * step) < step
                group = [
                    jnp.where(keep, a + pltpu.roll(a, 8 - step, 0), b + pltpu.roll(b, step, 0))
                    for a, b in zip(group[:step], group[step:])
                ]
            sums = jnp.sum(group[0], axis=1, keepdims=True)
            part = jnp.where(lane8 == sub8 + first, sums, 0.0)
            spread = part if spread is None else spread + part
        return jnp.sum(spread, axis=0, keepdims=True)

    def send_sums(which, values):
        packed = pack(values)
        sent[which] = packed
        slots[which, me] = packed

        def send(px, py):
            pltpu.make_async_remote_copy(
                src_ref=sent.at[which], dst_ref=slots.at[which, me],
                send_sem=sum_send.at[which], recv_sem=sum_recv.at[which],
                device_id=(px, py), device_id_type=MESH).start()

        columns = [lax.rem(gy + k, ny) for k in range(ny)]

        def line(k, carry):
            px = lax.rem(gx + k, nx)
            for py in columns:
                send(px, py)
            return carry

        lax.fori_loop(1, nx, line, 0)
        for py in columns[1:]:
            send(gx, py)

    def take_sums(which, many):
        others = slots.at[which, pl.ds(0, count - 1)]
        pltpu.make_async_copy(others, others, sum_recv.at[which]).wait()
        total = jnp.sum(slots[which], axis=0)
        return [total[:, k:k + 1] for k in range(many)]

    def basis(b, core, window, last=True):
        v1 = apply_b(b, core, window)
        v2 = apply_b(v1, core, window)
        return (b, v1, v2, apply_half(v2, core)) if last else (b, v1, v2)

    def mix(c, v):
        return c[0] * v[0] + c[1] * v[1] + c[2] * v[2]

    def pairs(x, y):
        return [dot(x[0], y[0]), dot(x[0], y[1]), dot(x[1], y[1]),
                dot(x[1], y[2]), dot(x[2], y[2]),
                2.0 * dot(x[2], x[3]) if x is y
                else fold(x[2] * y[3] + y[2] * x[3])]

    def own_small(v):
        return [x[:rows, :cols] for x in v]

    each_halo(True, lambda copy: copy.wait_recv(), back=True)
    small_core = core_of("small")
    later = masked(field(0, "small"), "small")
    w = own_small(basis(value_rhs(later, 1, "small"), small_core, "small"))
    moments = pairs(w, w)
    pl.semaphore_wait(ready, nx - 1)
    send_sums(0, moments)
    each_halo(False, lambda copy: copy.wait_recv(), back=True)
    core = core_of("tall")
    later = masked(field(0, "tall"), "tall")
    v = basis(value_rhs(later, 1, "tall"), core, "tall", last=False)
    vs = [shrink(x, MARGIN) for x in v]
    c = solve_small(take_sums(0, 6))

    first_small = mix(c, vs)
    w = own_small(basis(value_rhs(first_small, 0, "small"), small_core, "small"))
    send_sums(1, pairs(w, w))
    first = mix(c, v)
    v = basis(value_rhs(first, 0, "tall"), core, "tall", last=False)
    v = [x[low_mid:high_mid] for x in v]
    face = faces(first_small)
    density = masked(field(4, "mid"), "mid")
    mid_core = core_of("mid")
    c = solve_small(take_sums(1, 6))
    second = mix(c, v)

    a = basis(advance(density, faces(second), "mid"), mid_core, "mid", last=False)
    a = [shrink(x, 8) for x in a]
    last = apply_half(a[2], small_core)
    inner = own_small(a + [last])
    families = [
        own_small(basis(advance(a[i], face, "small"), small_core, "small")) for i in range(3)]
    moments = pairs(inner, inner)
    for i in range(3):
        for j in range(i, 3):
            moments += pairs(families[i], families[j])
    send_sums(2, moments)
    both_ref[0] = second[8:8 + rows, :cols]
    each_halo(True, lambda copy: copy.wait_send())
    each_halo(False, lambda copy: copy.wait_send())
    for which in range(3):
        others = slots.at[which, pl.ds(0, count - 1)]
        pltpu.make_async_copy(others, others, sum_send.at[which]).wait()
    total = take_sums(2, len(moments))
    c = solve_small(total[:6])
    nu = [0.0] * 6
    at = 6
    for i in range(3):
        for j in range(i, 3):
            weight = c[i] * c[j] * (1.0 if i == j else 2.0)
            for k in range(6):
                nu[k] = nu[k] + weight * total[at + k]
            at += 6
    e = solve_small(nu)
    result = None
    for i in range(3):
        for k in range(3):
            part = (c[i] * e[k]) * families[i][k]
            result = part if result is None else result + part
    both_ref[1] = result


def solution(mesh):
    nx, ny = mesh.shape["gx"], mesh.shape["gy"]

    def shards(terminal, initial_density, density_guess, diagonal):
        rows, cols = terminal.shape
        tall = rows + 2 * MARGIN
        hbm = pl.BlockSpec(memory_space=pl.ANY)
        vmem = pl.BlockSpec(memory_space=pltpu.VMEM)
        shape = jax.ShapeDtypeStruct((rows, cols), jnp.float32)
        both = pl.pallas_call(
            functools.partial(kernel, nx, ny),
            out_shape=jax.ShapeDtypeStruct((2, rows, cols), jnp.float32),
            in_specs=[hbm] * 4,
            out_specs=vmem,
            scratch_shapes=[
                pltpu.VMEM((5, tall, cols), jnp.float32),
                pltpu.VMEM((5, tall, LANES), jnp.float32),
                pltpu.VMEM((5, tall, LANES), jnp.float32),
                pltpu.VMEM((3, 1, LANES), jnp.float32),
                pltpu.VMEM((3, nx * ny, 1, LANES), jnp.float32),
                pltpu.SemaphoreType.DMA((8, 3)),
                pltpu.SemaphoreType.DMA((8, 3)),
                pltpu.SemaphoreType.DMA((5,)),
                pltpu.SemaphoreType.DMA((3,)),
                pltpu.SemaphoreType.DMA((3,)),
                pltpu.SemaphoreType.REGULAR,
                pltpu.VMEM((tall, cols + LANES), jnp.float32),
                pltpu.VMEM((rows + 16, cols + LANES), jnp.float32),
                pltpu.VMEM((rows + 8, cols + LANES), jnp.float32),
            ],
            compiler_params=pltpu.CompilerParams(collective_id=0, has_side_effects=True),
        )(terminal, initial_density, density_guess, diagonal)
        return both[0], both[1]

    placed = (P("gx", "gy"), P("gx", "gy"), P(None, "gx", "gy"), P("gx", "gy"))
    return jax.shard_map(
        shards,
        mesh=mesh,
        in_specs=placed,
        out_specs=(P("gx", "gy"), P("gx", "gy")),
        check_vma=False,
    )
```

profile of v0, /device:TPU:0, one launch (start us, length us, event | category | flops | bytes accessed | tf_op | source)
XLA Modules:
  0.0 31.1 jit_solution(4191677057845004744)
XLA Ops:
  0.6 29.1 %shard_map.59 = f32[2,16,512]{2,1,0:T(8,128)} custom-call(f32[16,512]{1,0:T(8,128)} %term_ref.1, f32[16,512]{1,0:T(8,128)} %dens_ref.1, f32[2,16,512]{2,1,0:T(8,128)} %guess_ref.1, f32[16,512]{1,0:T(8,128)} %diag_ref.1), custom_call_target="tpu_custom_call" | custom-call | tf_op jit(solution)/shard_map/pallas_call | solution.py:382
  29.7 1.4 %slice_bitcast_fusion = (f32[16,512]{1,0:T(8,128)}, f32[16,512]{1,0:T(8,128)}) fusion(f32[2,16,512]{2,1,0:T(8,128)} %shard_map.59), kind=kLoop, calls=%fused_computation | loop fusion | bytes 131072 | tf_op jit(solution)/shard_map/squeeze | solution.py:405
where the time goes:
time: 31.4 us; the launch traced here: 31.1 us
  Pallas kernels  29.1 us (93%)
  local copies, waits for them, and re-layouts  1.41 us (4%)
  between operations  0.64 us (2%)
    pallas_call x1, Pallas kernels, shards(): pl.pallas_call(functools.partial(kernel, nx, ny), out_shape=jax.ShapeDtyp...  29.1 us
    squeeze x1, local copies, waits for them, and re-layouts, shards(): return (both[0], both[1])  1.41 us

commit v1 on v0

--- a/solution.py
+++ b/solution.py
@@ -400,8 +400,8 @@
                 pltpu.VMEM((rows + 16, cols + LANES), jnp.float32),
                 pltpu.VMEM((rows + 8, cols + LANES), jnp.float32),
             ],
-            compiler_params=pltpu.CompilerParams(collective_id=0, has_side_effects=True),
-        )(terminal, initial_density, density_guess, diagonal)
+            compiler_params=pltpu.CompilerParams(collective_id=0, has_side_effects=True, vmem_limit_bytes=4 * 1024 * 1024),
+        )(*[pltpu.with_memory_space_constraint(x, pltpu.HBM) for x in (terminal, initial_density, density_guess, diagonal)])
         return both[0], both[1]
 
     placed = (P("gx", "gy"), P("gx", "gy"), P(None, "gx", "gy"), P("gx", "gy"))

time: 31.4 us -> 29.9 us (0.952)
  local copies, waits for them, and re-layouts: 1.41 us -> 0.63 us
  Pallas kernels: 29.1 us -> 28.5 us
    squeeze x1, local copies, waits for them, and re-layouts: 1.41 us -> 0.63 us  [shards(): return (both[0], both[1])]
    pallas_call x1, Pallas kernels: 29.1 us -> 28.5 us  [shards(): pl.pallas_call(functools.partial(kernel, nx, ny), out_shape=jax.ShapeDtyp...]
where the time goes in v1:
time: 29.9 us; the launch traced here: 29.7 us
  Pallas kernels  28.5 us (95%)
  between operations  0.64 us (2%)
  local copies, waits for them, and re-layouts  0.63 us (2%)
    pallas_call x1, Pallas kernels, shards(): pl.pallas_call(functools.partial(kernel, nx, ny), out_shape=jax.ShapeDtyp...  28.5 us
    squeeze x1, local copies, waits for them, and re-layouts, shards(): return (both[0], both[1])  0.63 us

profile of v1, /device:TPU:0, one launch (start us, length us, event | category | flops | bytes accessed | tf_op | source)
XLA Modules:
  0.0 29.7 jit_solution(1641842111784602472)
XLA Ops:
  0.6 28.5 %shard_map.59 = f32[2,16,512]{2,1,0:T(8,128)S(1)} custom-call(f32[16,512]{1,0:T(8,128)} %term_ref.1, f32[16,512]{1,0:T(8,128)} %dens_ref.1, f32[2,16,512]{2,1,0:T(8,128)} %guess_ref.1, f32[16,512]{1,0:T(8,128)} %diag_ref.1), custom_call_target="tpu_custom_call" | custom-call | tf_op jit(solution)/shard_map/pallas_call | solution.py:382
  29.1 0.6 %slice_bitcast_fusion = (f32[16,512]{1,0:T(8,128)}, f32[16,512]{1,0:T(8,128)}) fusion(f32[2,16,512]{2,1,0:T(8,128)S(1)} %shard_map.59), kind=kLoop, calls=%fused_computation | loop fusion | bytes 131072 | tf_op jit(solution)/shard_map/squeeze | solution.py:405

commit v2 on v1

--- a/solution.py
+++ b/solution.py
@@ -233,12 +233,14 @@
         own_part = (inv_step / SCALE) * later - (0.5 / SCALE) * hamiltonian(later)
         return scaled[window][...] * own_part + guess
 
-    def fold(p):
-        parts = [p[i:i + 8, j:j + LANES] for i in range(0, rows, 8) for j in range(0, cols, LANES)]
+    def tree(parts):
         while len(parts) > 1:
             odd = parts[len(parts) // 2 * 2:]
             parts = [parts[i] + parts[i + 1] for i in range(0, len(parts) - 1, 2)] + odd
         return parts[0]
+
+    def fold(p):
+        return tree([p[i:i + 8, j:j + LANES] for i in range(0, rows, 8) for j in range(0, cols, LANES)])
 
     def dot(x, y):
         return fold(x * y)
@@ -273,31 +275,34 @@
                 send_sem=sum_send.at[which], recv_sem=sum_recv.at[which],
                 device_id=(px, py), device_id_type=MESH).start()
 
-        columns = [lax.rem(gy + k, ny) for k in range(ny)]
-
         def line(k, carry):
             px = lax.rem(gx + k, nx)
-            for py in columns:
-                send(px, py)
+            for j in range(ny):
+                send(px, jnp.where(2 * gy < ny, ny - 1 - j, j))
             return carry
 
         lax.fori_loop(1, nx, line, 0)
-        for py in columns[1:]:
-            send(gx, py)
+        for k in range(1, ny):
+            send(gx, lax.rem(gy + k, ny))
 
     def take_sums(which, many):
         others = slots.at[which, pl.ds(0, count - 1)]
         pltpu.make_async_copy(others, others, sum_recv.at[which]).wait()
-        total = jnp.sum(slots[which], axis=0)
-        return [total[:, k:k + 1] for k in range(many)]
+        total = jnp.broadcast_to(tree([slots[which, k] for k in range(count)]), (8, LANES))
+        return [jnp.broadcast_to(total[:, k:k + 1], (8, LANES)) for k in range(many)]
 
     def basis(b, core, window, last=True):
         v1 = apply_b(b, core, window)
         v2 = apply_b(v1, core, window)
         return (b, v1, v2, apply_half(v2, core)) if last else (b, v1, v2)
 
+    def spread(tile, like):
+        wide_tile = jnp.concatenate([tile] * (like.shape[1] // LANES), axis=1)
+        return jnp.concatenate([wide_tile] * (like.shape[0] // 8), axis=0)
+
     def mix(c, v):
-        return c[0] * v[0] + c[1] * v[1] + c[2] * v[2]
+        parts = [spread(a, x) * x for a, x in zip(c, v)]
+        return (parts[0] + parts[1]) + parts[2]
 
     def pairs(x, y):
         return [dot(x[0], y[0]), dot(x[0], y[1]), dot(x[1], y[1]),
@@ -353,20 +358,14 @@
         pltpu.make_async_copy(others, others, sum_send.at[which]).wait()
     total = take_sums(2, len(moments))
     c = solve_small(total[:6])
-    nu = [0.0] * 6
-    at = 6
-    for i in range(3):
-        for j in range(i, 3):
-            weight = c[i] * c[j] * (1.0 if i == j else 2.0)
-            for k in range(6):
-                nu[k] = nu[k] + weight * total[at + k]
-            at += 6
+    picks = [(i, j) for i in range(3) for j in range(i, 3)]
+    weights = [c[i] * c[j] * (1.0 if i == j else 2.0) for i, j in picks]
+    nu = [
+        tree([weight * total[6 + 6 * at + k] for at, weight in enumerate(weights)])
+        for k in range(6)
+    ]
     e = solve_small(nu)
-    result = None
-    for i in range(3):
-        for k in range(3):
-            part = (c[i] * e[k]) * families[i][k]
-            result = part if result is None else result + part
+    result = mix(e, [mix(c, [families[i][k] for i in range(3)]) for k in range(3)])
     both_ref[1] = result
 
 

time: 29.9 us -> 27.6 us (0.923)
  Pallas kernels: 28.5 us -> 26.1 us
    pallas_call x1, Pallas kernels: 28.5 us -> 26.1 us  [shards(): pl.pallas_call(functools.partial(kernel, nx, ny), out_shape=jax.ShapeDtyp...]
where the time goes in v2:
time: 27.6 us; the launch traced here: 27.4 us
  Pallas kernels  26.1 us (95%)
  between operations  0.64 us (2%)
  local copies, waits for them, and re-layouts  0.63 us (2%)
    pallas_call x1, Pallas kernels, shards(): pl.pallas_call(functools.partial(kernel, nx, ny), out_shape=jax.ShapeDtyp...  26.1 us
    squeeze x1, local copies, waits for them, and re-layouts, shards(): return (both[0], both[1])  0.63 us

profile of v2, /device:TPU:0, one launch (start us, length us, event | category | flops | bytes accessed | tf_op | source)
XLA Modules:
  0.0 27.4 jit_solution(3743574549368657291)
XLA Ops:
  0.6 26.1 %shard_map.59 = f32[2,16,512]{2,1,0:T(8,128)S(1)} custom-call(f32[16,512]{1,0:T(8,128)} %term_ref.1, f32[16,512]{1,0:T(8,128)} %dens_ref.1, f32[2,16,512]{2,1,0:T(8,128)} %guess_ref.1, f32[16,512]{1,0:T(8,128)} %diag_ref.1), custom_call_target="tpu_custom_call" | custom-call | tf_op jit(solution)/shard_map/pallas_call | solution.py:381
  26.7 0.6 %slice_bitcast_fusion = (f32[16,512]{1,0:T(8,128)}, f32[16,512]{1,0:T(8,128)}) fusion(f32[2,16,512]{2,1,0:T(8,128)S(1)} %shard_map.59), kind=kLoop, calls=%fused_computation | loop fusion | bytes 131072 | tf_op jit(solution)/shard_map/squeeze | solution.py:404

commit v3 on v2

--- a/solution.py
+++ b/solution.py
@@ -50,7 +50,7 @@
 
 
 def kernel(nx, ny, term_ref, dens_ref, guess_ref, diag_ref, both_ref,
-           main, left, right, sent, slots, halo_send, halo_recv, own_sem, sum_send, sum_recv,
+           main, left, right, sent, slots, sizes, halo_send, halo_recv, own_sem, sum_send, sum_recv,
            ready, scaled_tall, scaled_mid, scaled_small):
     rows, cols = term_ref.shape
     gx = lax.axis_index("gx")
@@ -94,7 +94,7 @@
 
     here = pl.ds(MARGIN, rows)
     own = [
-        pltpu.make_async_copy(source, main.at[at, here], own_sem.at[at])
+        pltpu.make_async_copy(source, main.at[at, here], own_sem)
         for at, source in enumerate(
             (term_ref, diag_ref, guess_ref.at[1], guess_ref.at[0], dens_ref))
     ]
@@ -124,8 +124,7 @@
     scaled_mid[...] = jnp.where(mask_of(rows + 16, False, 8), SCALE, 0.0)
     scaled_small[...] = jnp.where(mask_of(rows + 8, True, 4), SCALE, 0.0)
 
-    for copy in own:
-        copy.wait()
+    pltpu.make_async_copy(main.at[:, here], main.at[:, here], own_sem).wait()
     pl.semaphore_wait(barrier, greeted)
 
     def pieces(dr):
@@ -153,20 +152,44 @@
         return pltpu.make_async_remote_copy(
             src_ref=main.at[pl.ds(first, many), src_rows, src_cols],
             dst_ref=buf.at[pl.ds(first, many), dst_rows, :],
-            send_sem=halo_send.at[d, piece], recv_sem=halo_recv.at[d, piece],
+            send_sem=halo_send, recv_sem=halo_recv.at[0 if piece == 0 else 1],
             device_id=(gx + dr, gy + dc), device_id_type=MESH)
 
-    def each_halo(near, act, back=False):
+    def start_halo(near):
         for d, (dr, dc) in enumerate(DIRECTIONS):
-            @pl.when(inside(-dr, -dc) if back else inside(dr, dc))
+            @pl.when(inside(dr, dc))
             def _():
                 for piece in [0] if near else range(1, len(pieces(dr))):
-                    act(halo(d, piece))
-
-    each_halo(True, lambda copy: copy.start())
+                    halo(d, piece).start()
+
+    def tiles(ends, sides, near):
+        total = 0
+        for dr, dc in ((1, 0), (0, 1), (1, 1)):
+            times = (ends if dr else 1) * (sides if dc else 1)
+            for at, (_, many, _, size) in enumerate(pieces(dr)):
+                if near is None or (at == 0) == near:
+                    total += times * many * (size // 8) * (1 if dc else cols // LANES)
+        return total
+
+    def beside_count(here_at, size):
+        return jnp.where(here_at > 0, 1, 0) + jnp.where(here_at < size - 1, 1, 0)
+
+    def wait_halo(sem, near):
+        for ends in range(min(1, nx - 1), min(2, nx - 1) + 1):
+            for sides in range(min(1, ny - 1), min(2, ny - 1) + 1):
+                many = tiles(ends, sides, near)
+                if many == 0:
+                    continue
+
+                @pl.when((beside_count(gx, nx) == ends) & (beside_count(gy, ny) == sides))
+                def _():
+                    span = sizes.at[pl.ds(0, many)]
+                    pltpu.make_async_copy(span, span, sem).wait()
+
+    start_halo(True)
     for k in range(1, nx):
         pl.semaphore_signal(ready, inc=1, device_id=across(k), device_id_type=MESH)
-    each_halo(False, lambda copy: copy.start())
+    start_halo(False)
 
     def shrink(x, start):
         sub = lax.broadcasted_iota(jnp.int32, (8, x.shape[1]), 0)
@@ -272,7 +295,7 @@
         def send(px, py):
             pltpu.make_async_remote_copy(
                 src_ref=sent.at[which], dst_ref=slots.at[which, me],
-                send_sem=sum_send.at[which], recv_sem=sum_recv.at[which],
+                send_sem=sum_send, recv_sem=sum_recv.at[which % 2],
                 device_id=(px, py), device_id_type=MESH).start()
 
         def line(k, carry):
@@ -287,7 +310,7 @@
 
     def take_sums(which, many):
         others = slots.at[which, pl.ds(0, count - 1)]
-        pltpu.make_async_copy(others, others, sum_recv.at[which]).wait()
+        pltpu.make_async_copy(others, others, sum_recv.at[which % 2]).wait()
         total = jnp.broadcast_to(tree([slots[which, k] for k in range(count)]), (8, LANES))
         return [jnp.broadcast_to(total[:, k:k + 1], (8, LANES)) for k in range(many)]
 
@@ -313,14 +336,14 @@
     def own_small(v):
         return [x[:rows, :cols] for x in v]
 
-    each_halo(True, lambda copy: copy.wait_recv(), back=True)
+    wait_halo(halo_recv.at[0], True)
     small_core = core_of("small")
     later = masked(field(0, "small"), "small")
     w = own_small(basis(value_rhs(later, 1, "small"), small_core, "small"))
     moments = pairs(w, w)
     pl.semaphore_wait(ready, nx - 1)
     send_sums(0, moments)
-    each_halo(False, lambda copy: copy.wait_recv(), back=True)
+    wait_halo(halo_recv.at[1], False)
     core = core_of("tall")
     later = masked(field(0, "tall"), "tall")
     v = basis(value_rhs(later, 1, "tall"), core, "tall", last=False)
@@ -351,11 +374,9 @@
             moments += pairs(families[i], families[j])
     send_sums(2, moments)
     both_ref[0] = second[8:8 + rows, :cols]
-    each_halo(True, lambda copy: copy.wait_send())
-    each_halo(False, lambda copy: copy.wait_send())
-    for which in range(3):
-        others = slots.at[which, pl.ds(0, count - 1)]
-        pltpu.make_async_copy(others, others, sum_send.at[which]).wait()
+    wait_halo(halo_send, None)
+    others = slots.at[:, pl.ds(0, count - 1)]
+    pltpu.make_async_copy(others, others, sum_send).wait()
     total = take_sums(2, len(moments))
     c = solve_small(total[:6])
     picks = [(i, j) for i in range(3) for j in range(i, 3)]
@@ -389,11 +410,12 @@
                 pltpu.VMEM((5, tall, LANES), jnp.float32),
                 pltpu.VMEM((3, 1, LANES), jnp.float32),
                 pltpu.VMEM((3, nx * ny, 1, LANES), jnp.float32),
-                pltpu.SemaphoreType.DMA((8, 3)),
-                pltpu.SemaphoreType.DMA((8, 3)),
-                pltpu.SemaphoreType.DMA((5,)),
-                pltpu.SemaphoreType.DMA((3,)),
-                pltpu.SemaphoreType.DMA((3,)),
+                pltpu.VMEM((5 * 4 * (rows // 8 + 2) * (cols // LANES + 2), 8, LANES), jnp.float32),
+                pltpu.SemaphoreType.DMA,
+                pltpu.SemaphoreType.DMA((2,)),
+                pltpu.SemaphoreType.DMA,
+                pltpu.SemaphoreType.DMA,
+                pltpu.SemaphoreType.DMA((2,)),
                 pltpu.SemaphoreType.REGULAR,
                 pltpu.VMEM((tall, cols + LANES), jnp.float32),
                 pltpu.VMEM((rows + 16, cols + LANES), jnp.float32),

time: 27.6 us -> 27.1 us (0.982)
  Pallas kernels: 26.1 us -> 25.6 us
    pallas_call x1, Pallas kernels: 26.1 us -> 25.6 us  [shards(): pl.pallas_call(functools.partial(kernel, nx, ny), out_shape=jax.ShapeDtyp...]
where the time goes in v3:
time: 27.1 us; the launch traced here: 26.9 us
  Pallas kernels  25.6 us (94%)
  between operations  0.64 us (2%)
  local copies, waits for them, and re-layouts  0.63 us (2%)
    pallas_call x1, Pallas kernels, shards(): pl.pallas_call(functools.partial(kernel, nx, ny), out_shape=jax.ShapeDtyp...  25.6 us
    squeeze x1, local copies, waits for them, and re-layouts, shards(): return (both[0], both[1])  0.63 us

profile of v3, /device:TPU:0, one launch (start us, length us, event | category | flops | bytes accessed | tf_op | source)
XLA Modules:
  0.0 26.9 jit_solution(17493585325400221570)
XLA Ops:
  0.6 25.6 %shard_map.59 = f32[2,16,512]{2,1,0:T(8,128)S(1)} custom-call(f32[16,512]{1,0:T(8,128)} %term_ref.1, f32[16,512]{1,0:T(8,128)} %dens_ref.1, f32[2,16,512]{2,1,0:T(8,128)} %guess_ref.1, f32[16,512]{1,0:T(8,128)} %diag_ref.1), custom_call_target="tpu_custom_call" | custom-call | tf_op jit(solution)/shard_map/pallas_call | solution.py:402
  26.3 0.6 %slice_bitcast_fusion = (f32[16,512]{1,0:T(8,128)}, f32[16,512]{1,0:T(8,128)}) fusion(f32[2,16,512]{2,1,0:T(8,128)S(1)} %shard_map.59), kind=kLoop, calls=%fused_computation | loop fusion | bytes 131072 | tf_op jit(solution)/shard_map/squeeze | solution.py:426

commit v4 on v3

--- a/solution.py
+++ b/solution.py
@@ -19,7 +19,7 @@
 SCALE = 0.25
 SHIFT = 5.5
 
-DIRECTIONS = [(r, c) for r in (-1, 0, 1) for c in (-1, 0, 1) if (r, c) != (0, 0)]
+DIRECTIONS = [(r, c) for r in (-1, 1) for c in (-1, 1)] + [(-1, 0), (1, 0), (0, -1), (0, 1)]
 TINY = 2e-7
 
 
@@ -50,7 +50,7 @@
 
 
 def kernel(nx, ny, term_ref, dens_ref, guess_ref, diag_ref, both_ref,
-           main, left, right, sent, slots, sizes, halo_send, halo_recv, own_sem, sum_send, sum_recv,
+           main, left, right, rim, edge, edge_left, edge_right, sent, slots, sizes, halo_send, halo_recv, own_sem, sum_send, sum_recv,
            ready, scaled_tall, scaled_mid, scaled_small):
     rows, cols = term_ref.shape
     gx = lax.axis_index("gx")
@@ -78,19 +78,20 @@
 
     barrier = pltpu.get_barrier_semaphore()
     greeted = nx + ny - 2
+    for dr, dc in DIRECTIONS:
+        if dr != 0 and dc != 0:
+            there = inside(dr, dc)
+            greeted = greeted + jnp.where(there, 1, 0)
+
+            @pl.when(there)
+            def _():
+                pl.semaphore_signal(
+                    barrier, inc=1, device_id=(gx + dr, gy + dc), device_id_type=MESH)
+
     for k in range(1, nx):
         pl.semaphore_signal(barrier, inc=1, device_id=across(k), device_id_type=MESH)
     for k in range(1, ny):
         pl.semaphore_signal(barrier, inc=1, device_id=along(k), device_id_type=MESH)
-    for dr, dc in DIRECTIONS:
-        if dr != 0 and dc != 0:
-            there = inside(dr, dc)
-            greeted = greeted + jnp.where(there, 1, 0)
-
-            @pl.when(there)
-            def _():
-                pl.semaphore_signal(
-                    barrier, inc=1, device_id=(gx + dr, gy + dc), device_id_type=MESH)
 
     here = pl.ds(MARGIN, rows)
     own = [
@@ -125,12 +126,16 @@
     scaled_small[...] = jnp.where(mask_of(rows + 8, True, 4), SCALE, 0.0)
 
     pltpu.make_async_copy(main.at[:, here], main.at[:, here], own_sem).wait()
+    for part in range(2):
+        for a in range(3):
+            rim[part, 0, a] = main[a, MARGIN + 4 * part:MARGIN + 4 * part + 4]
+            rim[part, 1, a] = main[a, MARGIN + rows - 4 * part - 4:MARGIN + rows - 4 * part]
     pl.semaphore_wait(barrier, greeted)
 
     def pieces(dr):
         if dr == 0:
             return [(0, 3, 0, rows), (3, 2, 0, rows)]
-        return [(0, 3, 0, 8), (0, 4, 8, 8), (3, 2, 0, 8)]
+        return [(0, 3, 0, 4), (0, 3, 4, 4), (0, 4, 8, 8), (3, 2, 0, 8)]
 
     def halo(d, piece):
         dr, dc = DIRECTIONS[d]
@@ -144,14 +149,17 @@
             src_rows = pl.ds(MARGIN + out, size)
             dst_rows = pl.ds(MARGIN + rows + out, size)
         if dc == 0:
-            src_cols, buf = pl.ds(0, cols), main
+            src_cols, buf, rim_buf = pl.ds(0, cols), main, edge
         elif dc == 1:
-            src_cols, buf = pl.ds(cols - LANES, LANES), left
+            src_cols, buf, rim_buf = pl.ds(cols - LANES, LANES), left, edge_left
         else:
-            src_cols, buf = pl.ds(0, LANES), right
+            src_cols, buf, rim_buf = pl.ds(0, LANES), right, edge_right
+        src, dst = main.at[pl.ds(first, many), src_rows, src_cols], buf.at[pl.ds(first, many), dst_rows, :]
+        if size == 4:
+            src = rim.at[out // 4, 1 if dr == 1 else 0, :, :, src_cols]
+            dst = rim_buf.at[out // 4, 1 if dr == 1 else 0]
         return pltpu.make_async_remote_copy(
-            src_ref=main.at[pl.ds(first, many), src_rows, src_cols],
-            dst_ref=buf.at[pl.ds(first, many), dst_rows, :],
+            src_ref=src, dst_ref=dst,
             send_sem=halo_send, recv_sem=halo_recv.at[0 if piece == 0 else 1],
             device_id=(gx + dr, gy + dc), device_id_type=MESH)
 
@@ -168,7 +176,7 @@
             times = (ends if dr else 1) * (sides if dc else 1)
             for at, (_, many, _, size) in enumerate(pieces(dr)):
                 if near is None or (at == 0) == near:
-                    total += times * many * (size // 8) * (1 if dc else cols // LANES)
+                    total += times * many * (size // 4) * (1 if dc else cols // LANES)
         return total
 
     def beside_count(here_at, size):
@@ -196,16 +204,32 @@
         ends = jnp.where(sub < 4, x[start + rows:start + rows + 8], x[start - 8:start])
         return jnp.concatenate([x[start:start + rows], ends], axis=0)
 
+    def joined(x, from_right, from_left):
+        lane = lax.broadcasted_iota(jnp.int32, from_right.shape, 1)
+        return jnp.concatenate([x, jnp.where(lane < half, from_right, from_left)], axis=1)
+
     def strip(a, begin, end):
-        lane = lax.broadcasted_iota(jnp.int32, (end - begin, LANES), 1)
-        edge = jnp.where(lane < half, right[a, begin:end], left[a, begin:end])
-        return jnp.concatenate([main[a, begin:end], edge], axis=1)
+        return joined(main[a, begin:end], right[a, begin:end], left[a, begin:end])
+
+    def rims(a, one, other):
+        return joined(*(
+            jnp.concatenate([buf[part, side, a] for part, side in (one, other)], axis=0)
+            for buf in (edge, edge_right, edge_left)))
 
     def field(a, window):
+        if a > 2:
+            if window == "tall":
+                return strip(a, 0, tall)
+            x = strip(a, low_mid, high_mid)
+            return x if window == "mid" else shrink(x, 8)
+        own_rows = strip(a, MARGIN, MARGIN + rows)
+        if window == "small":
+            return jnp.concatenate([own_rows, rims(a, (0, 0), (0, 1))], axis=0)
+        above, below = rims(a, (1, 1), (0, 1)), rims(a, (0, 0), (1, 0))
+        x = [above, own_rows, below]
         if window == "tall":
-            return strip(a, 0, tall)
-        x = strip(a, low_mid, high_mid)
-        return x if window == "mid" else shrink(x, 8)
+            x = [strip(a, 0, low_mid)] + x + [strip(a, high_mid, tall)]
+        return jnp.concatenate(x, axis=0)
 
     def up(x):
         return pltpu.roll(x, 1, 0)
@@ -408,9 +432,13 @@
                 pltpu.VMEM((5, tall, cols), jnp.float32),
                 pltpu.VMEM((5, tall, LANES), jnp.float32),
                 pltpu.VMEM((5, tall, LANES), jnp.float32),
+                pltpu.VMEM((2, 2, 3, 4, cols), jnp.float32),
+                pltpu.VMEM((2, 2, 3, 4, cols), jnp.float32),
+                pltpu.VMEM((2, 2, 3, 4, LANES), jnp.float32),
+                pltpu.VMEM((2, 2, 3, 4, LANES), jnp.float32),
                 pltpu.VMEM((3, 1, LANES), jnp.float32),
                 pltpu.VMEM((3, nx * ny, 1, LANES), jnp.float32),
-                pltpu.VMEM((5 * 4 * (rows // 8 + 2) * (cols // LANES + 2), 8, LANES), jnp.float32),
+                pltpu.VMEM((10 * 4 * (rows // 8 + 2) * (cols // LANES + 2), 4, LANES), jnp.float32),
                 pltpu.SemaphoreType.DMA,
                 pltpu.SemaphoreType.DMA((2,)),
                 pltpu.SemaphoreType.DMA,

time: 27.1 us -> 25.6 us (0.945)
  Pallas kernels: 25.6 us -> 24.1 us
    pallas_call x1, Pallas kernels: 25.6 us -> 24.1 us  [shards(): pl.pallas_call(functools.partial(kernel, nx, ny), out_shape=jax.ShapeDtyp...]
where the time goes in v4:
time: 25.6 us; the launch traced here: 25.4 us
  Pallas kernels  24.1 us (94%)
  between operations  0.64 us (2%)
  local copies, waits for them, and re-layouts  0.63 us (2%)
    pallas_call x1, Pallas kernels, shards(): pl.pallas_call(functools.partial(kernel, nx, ny), out_shape=jax.ShapeDtyp...  24.1 us
    squeeze x1, local copies, waits for them, and re-layouts, shards(): return (both[0], both[1])  0.63 us

profile of v4, /device:TPU:0, one launch (start us, length us, event | category | flops | bytes accessed | tf_op | source)
XLA Modules:
  0.0 25.4 jit_solution(5283559838059897469)
XLA Ops:
  0.6 24.1 %shard_map.59 = f32[2,16,512]{2,1,0:T(8,128)S(1)} custom-call(f32[16,512]{1,0:T(8,128)} %term_ref.1, f32[16,512]{1,0:T(8,128)} %dens_ref.1, f32[2,16,512]{2,1,0:T(8,128)} %guess_ref.1, f32[16,512]{1,0:T(8,128)} %diag_ref.1), custom_call_target="tpu_custom_call" | custom-call | tf_op jit(solution)/shard_map/pallas_call | solution.py:426
  24.7 0.6 %slice_bitcast_fusion = (f32[16,512]{1,0:T(8,128)}, f32[16,512]{1,0:T(8,128)}) fusion(f32[2,16,512]{2,1,0:T(8,128)S(1)} %shard_map.59), kind=kLoop, calls=%fused_computation | loop fusion | bytes 131072 | tf_op jit(solution)/shard_map/squeeze | solution.py:454

commit v5 on v4

--- a/solution.py
+++ b/solution.py
@@ -126,20 +126,24 @@
     scaled_small[...] = jnp.where(mask_of(rows + 8, True, 4), SCALE, 0.0)
 
     pltpu.make_async_copy(main.at[:, here], main.at[:, here], own_sem).wait()
-    for part in range(2):
+    for part in range(3):
         for a in range(3):
             rim[part, 0, a] = main[a, MARGIN + 4 * part:MARGIN + 4 * part + 4]
             rim[part, 1, a] = main[a, MARGIN + rows - 4 * part - 4:MARGIN + rows - 4 * part]
     pl.semaphore_wait(barrier, greeted)
 
-    def pieces(dr):
+    def pieces(dr, stage):
         if dr == 0:
-            return [(0, 3, 0, rows), (3, 2, 0, rows)]
-        return [(0, 3, 0, 4), (0, 3, 4, 4), (0, 4, 8, 8), (3, 2, 0, 8)]
-
-    def halo(d, piece):
+            return [[(0, 3, 0, rows)], [], [(3, 2, 0, rows)]][stage]
+        return [
+            [(0, 3, 0, 4)],
+            [(0, 3, 4, 4), (1, 2, 8, 4), (0, 1, 8, 8)],
+            [(3, 2, 0, 8), (3, 1, 8, 8)],
+        ][stage]
+
+    def halo(d, stage, piece):
         dr, dc = DIRECTIONS[d]
-        first, many, out, size = pieces(dr)[piece]
+        first, many, out, size = piece
         if dr == 0:
             src_rows, dst_rows = here, here
         elif dr == 1:
@@ -154,38 +158,41 @@
             src_cols, buf, rim_buf = pl.ds(cols - LANES, LANES), left, edge_left
         else:
             src_cols, buf, rim_buf = pl.ds(0, LANES), right, edge_right
-        src, dst = main.at[pl.ds(first, many), src_rows, src_cols], buf.at[pl.ds(first, many), dst_rows, :]
+        src = main.at[pl.ds(first, many), src_rows, src_cols]
+        dst = buf.at[pl.ds(first, many), dst_rows, :]
         if size == 4:
-            src = rim.at[out // 4, 1 if dr == 1 else 0, :, :, src_cols]
-            dst = rim_buf.at[out // 4, 1 if dr == 1 else 0]
+            side = 1 if dr == 1 else 0
+            src = rim.at[out // 4, side, pl.ds(first, many), :, src_cols]
+            dst = rim_buf.at[out // 4, side, pl.ds(first, many)]
         return pltpu.make_async_remote_copy(
             src_ref=src, dst_ref=dst,
-            send_sem=halo_send, recv_sem=halo_recv.at[0 if piece == 0 else 1],
+            send_sem=halo_send, recv_sem=halo_recv.at[stage],
             device_id=(gx + dr, gy + dc), device_id_type=MESH)
 
-    def start_halo(near):
+    def start_halo(stage):
         for d, (dr, dc) in enumerate(DIRECTIONS):
-            @pl.when(inside(dr, dc))
-            def _():
-                for piece in [0] if near else range(1, len(pieces(dr))):
-                    halo(d, piece).start()
-
-    def tiles(ends, sides, near):
+            if pieces(dr, stage):
+                @pl.when(inside(dr, dc))
+                def _():
+                    for piece in pieces(dr, stage):
+                        halo(d, stage, piece).start()
+
+    def tiles(ends, sides, stages):
         total = 0
         for dr, dc in ((1, 0), (0, 1), (1, 1)):
             times = (ends if dr else 1) * (sides if dc else 1)
-            for at, (_, many, _, size) in enumerate(pieces(dr)):
-                if near is None or (at == 0) == near:
+            for stage in stages:
+                for _, many, _, size in pieces(dr, stage):
                     total += times * many * (size // 4) * (1 if dc else cols // LANES)
         return total
 
     def beside_count(here_at, size):
         return jnp.where(here_at > 0, 1, 0) + jnp.where(here_at < size - 1, 1, 0)
 
-    def wait_halo(sem, near):
+    def wait_halo(sem, *stages):
         for ends in range(min(1, nx - 1), min(2, nx - 1) + 1):
             for sides in range(min(1, ny - 1), min(2, ny - 1) + 1):
-                many = tiles(ends, sides, near)
+                many = tiles(ends, sides, stages)
                 if many == 0:
                     continue
 
@@ -194,10 +201,11 @@
                     span = sizes.at[pl.ds(0, many)]
                     pltpu.make_async_copy(span, span, sem).wait()
 
-    start_halo(True)
+    start_halo(0)
     for k in range(1, nx):
         pl.semaphore_signal(ready, inc=1, device_id=across(k), device_id_type=MESH)
-    start_halo(False)
+    start_halo(1)
+    start_halo(2)
 
     def shrink(x, start):
         sub = lax.broadcasted_iota(jnp.int32, (8, x.shape[1]), 0)
@@ -227,8 +235,10 @@
             return jnp.concatenate([own_rows, rims(a, (0, 0), (0, 1))], axis=0)
         above, below = rims(a, (1, 1), (0, 1)), rims(a, (0, 0), (1, 0))
         x = [above, own_rows, below]
-        if window == "tall":
+        if window == "tall" and a == 0:
             x = [strip(a, 0, low_mid)] + x + [strip(a, high_mid, tall)]
+        elif window == "tall":
+            x = [rims(a, (2, 1), (2, 1))] + x + [rims(a, (2, 0), (2, 0))]
         return jnp.concatenate(x, axis=0)
 
     def up(x):
@@ -256,29 +266,42 @@
     def apply_half(v, core):
         return (0.5 * core) * v - SCALE * (down(v) + after(v))
 
-    def hamiltonian(u):
-        dx = u - up(u)
-        dy = u - before(u)
-        px, qx = jnp.maximum(dx, 0.0), jnp.minimum(dx, 0.0)
-        py, qy = jnp.maximum(dy, 0.0), jnp.minimum(dy, 0.0)
-        return (px * px + down(qx * qx)) + (py * py + after(qy * qy))
-
-    def faces(u):
-        sx = u - down(u)
-        sy = u - after(u)
+    def slopes(u):
+        back_x, back_y = u - up(u), u - before(u)
+        return back_x, down(back_x), back_y, after(back_y)
+
+    def hamiltonian(slope):
+        back_x, ahead_x, back_y, ahead_y = slope
+        px, qx = jnp.maximum(back_x, 0.0), jnp.minimum(ahead_x, 0.0)
+        py, qy = jnp.maximum(back_y, 0.0), jnp.minimum(ahead_y, 0.0)
+        return (px * px + qx * qx) + (py * py + qy * qy)
+
+    def falls(u):
+        return u - down(u), u - after(u)
+
+    def faces(fall):
+        sx, sy = fall
         return jnp.maximum(sx, 0.0), jnp.minimum(sx, 0.0), jnp.maximum(sy, 0.0), jnp.minimum(sy, 0.0)
 
-    def advance(m, face, window):
+    def ahead(m):
+        return m, down(m), after(m)
+
+    def unit(window):
+        return (1.0 / SCALE) * scaled[window][...]
+
+    def advance(m_ahead, face, ones):
+        m, below, beyond = m_ahead
         px, qx, py, qy = face
-        fx = px * m + qx * down(m)
-        fy = py * m + qy * after(m)
+        fx = px * m + qx * below
+        fy = py * m + qy * beyond
         net = (fx - up(fx)) + (fy - before(fy))
-        return scaled[window][...] * ((inv_step / SCALE) * m - (1.0 / SCALE) * net)
-
-    def value_rhs(later, level, window):
-        guess = masked(coupling * field(2 if level == 1 else 3, window), window)
-        own_part = (inv_step / SCALE) * later - (0.5 / SCALE) * hamiltonian(later)
-        return scaled[window][...] * own_part + guess
+        return inv_step * m - ones * net
+
+    def own_guess(level, window):
+        return masked(coupling * field(2 if level == 1 else 3, window), window)
+
+    def value_rhs(later, slope, guess, ones):
+        return (inv_step * later + guess) - (0.5 * ones) * hamiltonian(slope)
 
     def tree(parts):
         while len(parts) > 1:
@@ -360,45 +383,53 @@
     def own_small(v):
         return [x[:rows, :cols] for x in v]
 
-    wait_halo(halo_recv.at[0], True)
+    wait_halo(halo_recv.at[0], 0)
     small_core = core_of("small")
+    small_ones = unit("small")
     later = masked(field(0, "small"), "small")
-    w = own_small(basis(value_rhs(later, 1, "small"), small_core, "small"))
+    w = own_small(basis(
+        value_rhs(later, slopes(later), own_guess(1, "small"), small_ones), small_core, "small"))
     moments = pairs(w, w)
     pl.semaphore_wait(ready, nx - 1)
     send_sums(0, moments)
-    wait_halo(halo_recv.at[1], False)
-    core = core_of("tall")
+    wait_halo(halo_recv.at[1], 1)
+    core, ones = core_of("tall"), unit("tall")
     later = masked(field(0, "tall"), "tall")
-    v = basis(value_rhs(later, 1, "tall"), core, "tall", last=False)
+    v = basis(
+        value_rhs(later, slopes(later), own_guess(1, "tall"), ones), core, "tall", last=False)
     vs = [shrink(x, MARGIN) for x in v]
+    steep = list(zip(*[slopes(x) for x in vs]))
+    wait_halo(halo_recv.at[2], 2)
+    guess = own_guess(0, "small")
     c = solve_small(take_sums(0, 6))
 
     first_small = mix(c, vs)
-    w = own_small(basis(value_rhs(first_small, 0, "small"), small_core, "small"))
+    w = own_small(basis(
+        value_rhs(first_small, [mix(c, x) for x in steep], guess, small_ones), small_core, "small"))
     send_sums(1, pairs(w, w))
     first = mix(c, v)
-    v = basis(value_rhs(first, 0, "tall"), core, "tall", last=False)
+    v = basis(value_rhs(first, slopes(first), own_guess(0, "tall"), ones), core, "tall", last=False)
     v = [x[low_mid:high_mid] for x in v]
-    face = faces(first_small)
-    density = masked(field(4, "mid"), "mid")
-    mid_core = core_of("mid")
+    steep = list(zip(*[falls(x) for x in v]))
+    face = faces(falls(first_small))
+    density = ahead(masked(field(4, "mid"), "mid"))
+    mid_core, mid_ones = core_of("mid"), unit("mid")
     c = solve_small(take_sums(1, 6))
-    second = mix(c, v)
-
-    a = basis(advance(density, faces(second), "mid"), mid_core, "mid", last=False)
+
+    rhs = advance(density, faces([mix(c, x) for x in steep]), mid_ones)
+    a = basis(rhs, mid_core, "mid", last=False)
     a = [shrink(x, 8) for x in a]
     last = apply_half(a[2], small_core)
     inner = own_small(a + [last])
     families = [
-        own_small(basis(advance(a[i], face, "small"), small_core, "small")) for i in range(3)]
+        own_small(basis(advance(ahead(x), face, small_ones), small_core, "small")) for x in a]
     moments = pairs(inner, inner)
     for i in range(3):
         for j in range(i, 3):
             moments += pairs(families[i], families[j])
     send_sums(2, moments)
-    both_ref[0] = second[8:8 + rows, :cols]
-    wait_halo(halo_send, None)
+    both_ref[0] = mix(c, [x[8:8 + rows, :cols] for x in v])
+    wait_halo(halo_send, 0, 1, 2)
     others = slots.at[:, pl.ds(0, count - 1)]
     pltpu.make_async_copy(others, others, sum_send).wait()
     total = take_sums(2, len(moments))
@@ -432,15 +463,15 @@
                 pltpu.VMEM((5, tall, cols), jnp.float32),
                 pltpu.VMEM((5, tall, LANES), jnp.float32),
                 pltpu.VMEM((5, tall, LANES), jnp.float32),
-                pltpu.VMEM((2, 2, 3, 4, cols), jnp.float32),
-                pltpu.VMEM((2, 2, 3, 4, cols), jnp.float32),
-                pltpu.VMEM((2, 2, 3, 4, LANES), jnp.float32),
-                pltpu.VMEM((2, 2, 3, 4, LANES), jnp.float32),
+                pltpu.VMEM((3, 2, 3, 4, cols), jnp.float32),
+                pltpu.VMEM((3, 2, 3, 4, cols), jnp.float32),
+                pltpu.VMEM((3, 2, 3, 4, LANES), jnp.float32),
+                pltpu.VMEM((3, 2, 3, 4, LANES), jnp.float32),
                 pltpu.VMEM((3, 1, LANES), jnp.float32),
                 pltpu.VMEM((3, nx * ny, 1, LANES), jnp.float32),
                 pltpu.VMEM((10 * 4 * (rows // 8 + 2) * (cols // LANES + 2), 4, LANES), jnp.float32),
                 pltpu.SemaphoreType.DMA,
-                pltpu.SemaphoreType.DMA((2,)),
+                pltpu.SemaphoreType.DMA((3,)),
                 pltpu.SemaphoreType.DMA,
                 pltpu.SemaphoreType.DMA,
                 pltpu.SemaphoreType.DMA((2,)),

time: 25.6 us -> 25.4 us (level)
  no operation moved by 1% of the time
where the time goes in v5:
time: 25.4 us; the launch traced here: 25.2 us
  Pallas kernels  23.9 us (94%)
  between operations  0.64 us (3%)
  local copies, waits for them, and re-layouts  0.63 us (2%)
    pallas_call x1, Pallas kernels, shards(): pl.pallas_call(functools.partial(kernel, nx, ny), out_shape=jax.ShapeDtyp...  23.9 us
    squeeze x1, local copies, waits for them, and re-layouts, shards(): return (both[0], both[1])  0.63 us

profile of v5, /device:TPU:0, one launch (start us, length us, event | category | flops | bytes accessed | tf_op | source)
XLA Modules:
  0.0 25.2 jit_solution(17929695463199204888)
XLA Ops:
  0.6 23.9 %shard_map.59 = f32[2,16,512]{2,1,0:T(8,128)S(1)} custom-call(f32[16,512]{1,0:T(8,128)} %term_ref.1, f32[16,512]{1,0:T(8,128)} %dens_ref.1, f32[2,16,512]{2,1,0:T(8,128)} %guess_ref.1, f32[16,512]{1,0:T(8,128)} %diag_ref.1), custom_call_target="tpu_custom_call" | custom-call | tf_op jit(solution)/shard_map/pallas_call | solution.py:457
  24.6 0.6 %slice_bitcast_fusion = (f32[16,512]{1,0:T(8,128)}, f32[16,512]{1,0:T(8,128)}) fusion(f32[2,16,512]{2,1,0:T(8,128)S(1)} %shard_map.59), kind=kLoop, calls=%fused_computation | loop fusion | bytes 131072 | tf_op jit(solution)/shard_map/squeeze | solution.py:485

commit v6 on v5

--- a/solution.py
+++ b/solution.py
@@ -345,13 +345,13 @@
                 send_sem=sum_send, recv_sem=sum_recv.at[which % 2],
                 device_id=(px, py), device_id_type=MESH).start()
 
-        def line(k, carry):
-            px = lax.rem(gx + k, nx)
-            for j in range(ny):
-                send(px, jnp.where(2 * gy < ny, ny - 1 - j, j))
-            return carry
-
-        lax.fori_loop(1, nx, line, 0)
+        for begin in (2, 1):
+            def column(j, carry):
+                for k in range(begin, nx, 2):
+                    send(lax.rem(gx + k, nx), jnp.where(2 * gy < ny, ny - 1 - j, j))
+                return carry
+
+            lax.fori_loop(0, ny, column, 0)
         for k in range(1, ny):
             send(gx, lax.rem(gy + k, ny))
 

time: 25.4 us -> 25.2 us (level)
  no operation moved by 1% of the time
where the time goes in v6:
time: 25.2 us; the launch traced here: 25 us
  Pallas kernels  23.8 us (94%)
  between operations  0.64 us (3%)
  local copies, waits for them, and re-layouts  0.63 us (2%)
    pallas_call x1, Pallas kernels, shards(): pl.pallas_call(functools.partial(kernel, nx, ny), out_shape=jax.ShapeDtyp...  23.8 us
    squeeze x1, local copies, waits for them, and re-layouts, shards(): return (both[0], both[1])  0.63 us

profile of v6, /device:TPU:0, one launch (start us, length us, event | category | flops | bytes accessed | tf_op | source)
XLA Modules:
  0.0 25.0 jit_solution(11199790618286926908)
XLA Ops:
  0.6 23.8 %shard_map.59 = f32[2,16,512]{2,1,0:T(8,128)S(1)} custom-call(f32[16,512]{1,0:T(8,128)} %term_ref.1, f32[16,512]{1,0:T(8,128)} %dens_ref.1, f32[2,16,512]{2,1,0:T(8,128)} %guess_ref.1, f32[16,512]{1,0:T(8,128)} %diag_ref.1), custom_call_target="tpu_custom_call" | custom-call | tf_op jit(solution)/shard_map/pallas_call | solution.py:457
  24.4 0.6 %slice_bitcast_fusion = (f32[16,512]{1,0:T(8,128)}, f32[16,512]{1,0:T(8,128)}) fusion(f32[2,16,512]{2,1,0:T(8,128)S(1)} %shard_map.59), kind=kLoop, calls=%fused_computation | loop fusion | bytes 131072 | tf_op jit(solution)/shard_map/squeeze | solution.py:485

commit v7 on v6

--- a/solution.py
+++ b/solution.py
@@ -267,8 +267,7 @@
         return (0.5 * core) * v - SCALE * (down(v) + after(v))
 
     def slopes(u):
-        back_x, back_y = u - up(u), u - before(u)
-        return back_x, down(back_x), back_y, after(back_y)
+        return u - up(u), down(u) - u, u - before(u), after(u) - u
 
     def hamiltonian(slope):
         back_x, ahead_x, back_y, ahead_y = slope
@@ -289,12 +288,16 @@
     def unit(window):
         return (1.0 / SCALE) * scaled[window][...]
 
-    def advance(m_ahead, face, ones):
+    def advance(m_ahead, face, ones, face_behind=None):
         m, below, beyond = m_ahead
         px, qx, py, qy = face
         fx = px * m + qx * below
         fy = py * m + qy * beyond
-        net = (fx - up(fx)) + (fy - before(fy))
+        if face_behind is None:
+            fy_behind = before(fy)
+        else:
+            fy_behind = face_behind[0] * before(m) + face_behind[1] * m
+        net = (fx - up(fx)) + (fy - fy_behind)
         return inv_step * m - ones * net
 
     def own_guess(level, window):
@@ -347,7 +350,7 @@
 
         for begin in (2, 1):
             def column(j, carry):
-                for k in range(begin, nx, 2):
+                for k in sorted(range(begin, nx, 2), key=lambda k: min(k, nx - k)):
                     send(lax.rem(gx + k, nx), jnp.where(2 * gy < ny, ny - 1 - j, j))
                 return carry
 
@@ -412,6 +415,7 @@
     v = [x[low_mid:high_mid] for x in v]
     steep = list(zip(*[falls(x) for x in v]))
     face = faces(falls(first_small))
+    behind = before(face[2]), before(face[3])
     density = ahead(masked(field(4, "mid"), "mid"))
     mid_core, mid_ones = core_of("mid"), unit("mid")
     c = solve_small(take_sums(1, 6))
@@ -422,7 +426,9 @@
     last = apply_half(a[2], small_core)
     inner = own_small(a + [last])
     families = [
-        own_small(basis(advance(ahead(x), face, small_ones), small_core, "small")) for x in a]
+        own_small(basis(
+            advance(ahead(x), face, small_ones, behind if x is a[2] else None), small_core, "small"))
+        for x in a]
     moments = pairs(inner, inner)
     for i in range(3):
         for j in range(i, 3):

time: 25.2 us -> 25.1 us (level)
  no operation moved by 1% of the time
where the time goes in v7:
time: 25.1 us; the launch traced here: 24.9 us
  Pallas kernels  23.7 us (94%)
  between operations  0.64 us (3%)
  local copies, waits for them, and re-layouts  0.63 us (3%)
    pallas_call x1, Pallas kernels, shards(): pl.pallas_call(functools.partial(kernel, nx, ny), out_shape=jax.ShapeDtyp...  23.7 us
    squeeze x1, local copies, waits for them, and re-layouts, shards(): return (both[0], both[1])  0.63 us

profile of v7, /device:TPU:0, one launch (start us, length us, event | category | flops | bytes accessed | tf_op | source)
XLA Modules:
  0.0 24.9 jit_solution(4393255656104348947)
XLA Ops:
  0.6 23.7 %shard_map.59 = f32[2,16,512]{2,1,0:T(8,128)S(1)} custom-call(f32[16,512]{1,0:T(8,128)} %term_ref.1, f32[16,512]{1,0:T(8,128)} %dens_ref.1, f32[2,16,512]{2,1,0:T(8,128)} %guess_ref.1, f32[16,512]{1,0:T(8,128)} %diag_ref.1), custom_call_target="tpu_custom_call" | custom-call | tf_op jit(solution)/shard_map/pallas_call | solution.py:463
  24.3 0.6 %slice_bitcast_fusion = (f32[16,512]{1,0:T(8,128)}, f32[16,512]{1,0:T(8,128)}) fusion(f32[2,16,512]{2,1,0:T(8,128)S(1)} %shard_map.59), kind=kLoop, calls=%fused_computation | loop fusion | bytes 131072 | tf_op jit(solution)/shard_map/squeeze | solution.py:491

commit v8 on v7

--- a/solution.py
+++ b/solution.py
@@ -19,7 +19,8 @@
 SCALE = 0.25
 SHIFT = 5.5
 
-DIRECTIONS = [(r, c) for r in (-1, 1) for c in (-1, 1)] + [(-1, 0), (1, 0), (0, -1), (0, 1)]
+CORNERS = [(r, c) for r in (-1, 1) for c in (-1, 1)]
+DIRECTIONS = [(-1, 0), (1, 0)] + CORNERS + [(0, -1), (0, 1)]
 TINY = 2e-7
 
 
@@ -88,10 +89,10 @@
                 pl.semaphore_signal(
                     barrier, inc=1, device_id=(gx + dr, gy + dc), device_id_type=MESH)
 
+    for k in range(1, ny):
+        pl.semaphore_signal(barrier, inc=1, device_id=along(k), device_id_type=MESH)
     for k in range(1, nx):
         pl.semaphore_signal(barrier, inc=1, device_id=across(k), device_id_type=MESH)
-    for k in range(1, ny):
-        pl.semaphore_signal(barrier, inc=1, device_id=along(k), device_id_type=MESH)
 
     here = pl.ds(MARGIN, rows)
     own = [
@@ -127,7 +128,7 @@
 
     pltpu.make_async_copy(main.at[:, here], main.at[:, here], own_sem).wait()
     for part in range(3):
-        for a in range(3):
+        for a in range(4 if part == 2 else 3):
             rim[part, 0, a] = main[a, MARGIN + 4 * part:MARGIN + 4 * part + 4]
             rim[part, 1, a] = main[a, MARGIN + rows - 4 * part - 4:MARGIN + rows - 4 * part]
     pl.semaphore_wait(barrier, greeted)
@@ -138,7 +139,7 @@
         return [
             [(0, 3, 0, 4)],
             [(0, 3, 4, 4), (1, 2, 8, 4), (0, 1, 8, 8)],
-            [(3, 2, 0, 8), (3, 1, 8, 8)],
+            [(3, 2, 0, 8), (3, 1, 8, 4)],
         ][stage]
 
     def halo(d, stage, piece):
@@ -226,9 +227,10 @@
 
     def field(a, window):
         if a > 2:
+            x = strip(a, low_mid, high_mid)
             if window == "tall":
-                return strip(a, 0, tall)
-            x = strip(a, low_mid, high_mid)
+                return jnp.concatenate(
+                    [rims(a, (2, 1), (2, 1)), x, rims(a, (2, 0), (2, 0))], axis=0)
             return x if window == "mid" else shrink(x, 8)
         own_rows = strip(a, MARGIN, MARGIN + rows)
         if window == "small":
@@ -469,10 +471,10 @@
                 pltpu.VMEM((5, tall, cols), jnp.float32),
                 pltpu.VMEM((5, tall, LANES), jnp.float32),
                 pltpu.VMEM((5, tall, LANES), jnp.float32),
-                pltpu.VMEM((3, 2, 3, 4, cols), jnp.float32),
-                pltpu.VMEM((3, 2, 3, 4, cols), jnp.float32),
-                pltpu.VMEM((3, 2, 3, 4, LANES), jnp.float32),
-                pltpu.VMEM((3, 2, 3, 4, LANES), jnp.float32),
+                pltpu.VMEM((3, 2, 4, 4, cols), jnp.float32),
+                pltpu.VMEM((3, 2, 4, 4, cols), jnp.float32),
+                pltpu.VMEM((3, 2, 4, 4, LANES), jnp.float32),
+                pltpu.VMEM((3, 2, 4, 4, LANES), jnp.float32),
                 pltpu.VMEM((3, 1, LANES), jnp.float32),
                 pltpu.VMEM((3, nx * ny, 1, LANES), jnp.float32),
                 pltpu.VMEM((10 * 4 * (rows // 8 + 2) * (cols // LANES + 2), 4, LANES), jnp.float32),
@@ -486,7 +488,7 @@
                 pltpu.VMEM((rows + 16, cols + LANES), jnp.float32),
                 pltpu.VMEM((rows + 8, cols + LANES), jnp.float32),
             ],
-            compiler_params=pltpu.CompilerParams(collective_id=0, has_side_effects=True, vmem_limit_bytes=4 * 1024 * 1024),
+            compiler_params=pltpu.CompilerParams(collective_id=0, has_side_effects=True, vmem_limit_bytes=8 * 1024 * 1024),
         )(*[pltpu.with_memory_space_constraint(x, pltpu.HBM) for x in (terminal, initial_density, density_guess, diagonal)])
         return both[0], both[1]
 

time: 25.1 us -> 25.1 us (level)
  no operation moved by 1% of the time
where the time goes in v8:
time: 25.1 us; the launch traced here: 24.9 us
  Pallas kernels  23.6 us (94%)
  between operations  0.64 us (3%)
  local copies, waits for them, and re-layouts  0.63 us (3%)
    pallas_call x1, Pallas kernels, shards(): pl.pallas_call(functools.partial(kernel, nx, ny), out_shape=jax.ShapeDtyp...  23.6 us
    squeeze x1, local copies, waits for them, and re-layouts, shards(): return (both[0], both[1])  0.63 us

profile of v8, /device:TPU:0, one launch (start us, length us, event | category | flops | bytes accessed | tf_op | source)
XLA Modules:
  0.0 24.9 jit_solution(897844318221349926)
XLA Ops:
  0.6 23.6 %shard_map.59 = f32[2,16,512]{2,1,0:T(8,128)S(1)} custom-call(f32[16,512]{1,0:T(8,128)} %term_ref.1, f32[16,512]{1,0:T(8,128)} %dens_ref.1, f32[2,16,512]{2,1,0:T(8,128)} %guess_ref.1, f32[16,512]{1,0:T(8,128)} %diag_ref.1), custom_call_target="tpu_custom_call" | custom-call | tf_op jit(solution)/shard_map/pallas_call | solution.py:465
  24.3 0.6 %slice_bitcast_fusion = (f32[16,512]{1,0:T(8,128)}, f32[16,512]{1,0:T(8,128)}) fusion(f32[2,16,512]{2,1,0:T(8,128)S(1)} %shard_map.59), kind=kLoop, calls=%fused_computation | loop fusion | bytes 131072 | tf_op jit(solution)/shard_map/squeeze | solution.py:493

commit v9 on v8

--- a/solution.py
+++ b/solution.py
@@ -356,7 +356,7 @@
                     send(lax.rem(gx + k, nx), jnp.where(2 * gy < ny, ny - 1 - j, j))
                 return carry
 
-            lax.fori_loop(0, ny, column, 0)
+            lax.fori_loop(0, ny, column, 0, unroll=count <= 64)
         for k in range(1, ny):
             send(gx, lax.rem(gy + k, ny))
 

time: 25.1 us -> 25.1 us (level)
  no operation moved by 1% of the time
where the time goes in v9:
time: 25.1 us; the launch traced here: 24.9 us
  Pallas kernels  23.6 us (94%)
  between operations  0.64 us (3%)
  local copies, waits for them, and re-layouts  0.63 us (3%)
    pallas_call x1, Pallas kernels, shards(): pl.pallas_call(functools.partial(kernel, nx, ny), out_shape=jax.ShapeDtyp...  23.6 us
    squeeze x1, local copies, waits for them, and re-layouts, shards(): return (both[0], both[1])  0.63 us

profile of v9, /device:TPU:0, one launch (start us, length us, event | category | flops | bytes accessed | tf_op | source)
XLA Modules:
  0.0 24.9 jit_solution(2158105072097771956)
XLA Ops:
  0.6 23.6 %shard_map.59 = f32[2,16,512]{2,1,0:T(8,128)S(1)} custom-call(f32[16,512]{1,0:T(8,128)} %term_ref.1, f32[16,512]{1,0:T(8,128)} %dens_ref.1, f32[2,16,512]{2,1,0:T(8,128)} %guess_ref.1, f32[16,512]{1,0:T(8,128)} %diag_ref.1), custom_call_target="tpu_custom_call" | custom-call | tf_op jit(solution)/shard_map/pallas_call | solution.py:465
  24.3 0.6 %slice_bitcast_fusion = (f32[16,512]{1,0:T(8,128)}, f32[16,512]{1,0:T(8,128)}) fusion(f32[2,16,512]{2,1,0:T(8,128)S(1)} %shard_map.59), kind=kLoop, calls=%fused_computation | loop fusion | bytes 131072 | tf_op jit(solution)/shard_map/squeeze | solution.py:493

commit v10 on v9

--- a/solution.py
+++ b/solution.py
@@ -269,7 +269,8 @@
         return (0.5 * core) * v - SCALE * (down(v) + after(v))
 
     def slopes(u):
-        return u - up(u), down(u) - u, u - before(u), after(u) - u
+        back = u - up(u)
+        return back, down(back), u - before(u), after(u) - u
 
     def hamiltonian(slope):
         back_x, ahead_x, back_y, ahead_y = slope

time: 25.1 us -> 25.1 us (level)
  no operation moved by 1% of the time
where the time goes in v10:
time: 25.1 us; the launch traced here: 24.9 us
  Pallas kernels  23.6 us (94%)
  between operations  0.64 us (3%)
  local copies, waits for them, and re-layouts  0.63 us (3%)
    pallas_call x1, Pallas kernels, shards(): pl.pallas_call(functools.partial(kernel, nx, ny), out_shape=jax.ShapeDtyp...  23.6 us
    squeeze x1, local copies, waits for them, and re-layouts, shards(): return (both[0], both[1])  0.63 us

profile of v10, /device:TPU:0, one launch (start us, length us, event | category | flops | bytes accessed | tf_op | source)
XLA Modules:
  0.0 24.9 jit_solution(12840654320389280239)
XLA Ops:
  0.6 23.6 %shard_map.59 = f32[2,16,512]{2,1,0:T(8,128)S(1)} custom-call(f32[16,512]{1,0:T(8,128)} %term_ref.1, f32[16,512]{1,0:T(8,128)} %dens_ref.1, f32[2,16,512]{2,1,0:T(8,128)} %guess_ref.1, f32[16,512]{1,0:T(8,128)} %diag_ref.1), custom_call_target="tpu_custom_call" | custom-call | tf_op jit(solution)/shard_map/pallas_call | solution.py:466
  24.2 0.6 %slice_bitcast_fusion = (f32[16,512]{1,0:T(8,128)}, f32[16,512]{1,0:T(8,128)}) fusion(f32[2,16,512]{2,1,0:T(8,128)S(1)} %shard_map.59), kind=kLoop, calls=%fused_computation | loop fusion | bytes 131072 | tf_op jit(solution)/shard_map/squeeze | solution.py:494
